TPU v7x, 32 devices: a whole 2x2x4 slice. The times are simulated.
32 devices in a mesh: row: 8 (over z, y), col: 4 (over x, core).
Axes of the slice: x: 2, y: 2, z: 4, core: 2. Of those that a mesh axis runs over, the one named last changes fastest.
Arguments:
- embeddings: bfloat16 [5, 192, 2048], P(None, None, ('row', 'col')), may hold values from -6 to 6
- scale_weights: float32 [5], replicated, may hold values from 0.1 to 0.5
- vectors: bfloat16 [32, 2048], P(None, ('row', 'col')), may hold values from -6 to 6
Outputs:
- product: float32 [32, 2048], P(None, ('row', 'col'))
All inputs are finite; a program needn't handle non-finite values.
Results may differ from a plain program's by a relative error of at most 0.011.
Values may be sent and summed in bfloat16 or wider, within the bound.
A program may use at most 64 MiB of HBM per device.

v0:
```python
import math
import jax
import jax.numpy as jnp
from jax import lax
from jax.sharding import PartitionSpec as P

SHARP = 3.5


def prepare(embeddings, scale_weights):
    values = embeddings.astype(jnp.float32)
    units = values * lax.rsqrt(jnp.sum(values * values, axis=1, keepdims=True) + 1e-06)
    unit = lax.optimization_barrier(units.astype(jnp.bfloat16))
    weighted = (scale_weights[:, None, None] * unit.astype(jnp.float32)).astype(jnp.bfloat16)
    segments = embeddings.shape[2]
    return (weighted.reshape(-1, segments), unit.reshape(-1, segments))


def tile_terms(row_panel, column_panel, column_vectors, row_ids, column_ids, sharpness):
    cosine = lax.dot_general(
        row_panel, column_panel, (((0,), (0,)), ((), ())), preferred_element_type=jnp.float32
    )
    affinity = jnp.where(
        row_ids[:, None] == column_ids[None, :], jnp.zeros_like(cosine), jnp.exp(sharpness * cosine)
    )
    degree = jnp.sum(affinity, axis=1)
    numerator = lax.dot_general(
        column_vectors,
        affinity.astype(jnp.bfloat16),
        (((1,), (1,)), ((), ())),
        preferred_element_type=jnp.float32,
    )
    return (numerator, degree)


def blocked(row_panel, column_panel, column_vectors, row_ids, column_ids, sharpness):
    width = column_panel.shape[1]
    stride = math.gcd(width, 512)
    numerator = jnp.zeros((column_vectors.shape[0], row_panel.shape[1]), jnp.float32)
    degree = jnp.zeros((row_panel.shape[1],), jnp.float32)
    for offset in range(0, width, stride):
        extra_numerator, extra_degree = tile_terms(
            row_panel,
            column_panel[:, offset : offset + stride],
            column_vectors[:, offset : offset + stride],
            row_ids,
            column_ids[offset : offset + stride],
            sharpness,
        )
        numerator = numerator + extra_numerator
        degree = degree + extra_degree
    return (numerator, degree)


def shards(embeddings, scale_weights, vectors):
    segments = embeddings.shape[2]
    col_count = lax.axis_size("col")
    row_index = lax.axis_index("row")
    col_index = lax.axis_index("col")
    sharpness = SHARP * math.sqrt(embeddings.shape[1])
    weighted, unit = prepare(embeddings, scale_weights)

    def positions_of(panel):
        return jnp.arange(panel.shape[1], dtype=jnp.int32)

    own_panel = lax.all_gather(weighted, "col", axis=1, tiled=True)
    own_ids = row_index * (col_count * segments) + positions_of(own_panel)
    partner_panel, partner_vectors = (
        lax.all_gather(unit, "row", axis=1, tiled=True),
        lax.all_gather(vectors, "row", axis=1, tiled=True),
    )
    positions = positions_of(partner_panel)
    numerator, degree = blocked(
        own_panel,
        partner_panel,
        partner_vectors,
        own_ids,
        (positions // segments * col_count + col_index) * segments + positions % segments,
        sharpness,
    )
    numerator, degree = (
        lax.psum_scatter(numerator, "col", scatter_dimension=1, tiled=True),
        lax.psum_scatter(degree, "col", scatter_dimension=0, tiled=True),
    )
    return numerator / degree[None, :]


def solution(mesh):
    placed = (P(None, None, ("row", "col")), P(), P(None, ("row", "col")))
    return jax.shard_map(
        shards, mesh=mesh, in_specs=placed, out_specs=P(None, ("row", "col")), check_vma=False
    )
```

profile of v0, /device:TPU:0, one launch (start us, length us, event | category | flops | bytes accessed | tf_op | source)
XLA Modules:
  0.0 111.4 jit_solution(14193638312619526555)
XLA Ops:
  6.5 0.0 copy-start
  6.5 0.0 reduce-scatter.4.cloned.1.call-start
  6.5 1.1 fusion.2
  7.7 0.0 copy-done
  7.7 0.1 fusion.3
  7.8 0.1 copy.8
  7.9 0.2 reshape.43
  8.1 0.0 copy-start.2
  8.1 34.6 %all_gather.10 = bf16[960,512]{0,1:T(8,128)(2,1)S(1)} all-gather(bf16[960,64]{0,1:T(8,128)(2,1)S(1)} %reshape.43), channel_id=1, replica_groups=mesh['row'=8,'col'=4] {'row'}, dimensions={1}, use_global_device_ids=true | all-gather | bytes 1105920 | tf_op jit(solution)/shard_map/all_gather | solution.py:69
  42.7 0.0 copy-done.2
  42.7 0.1 multiply_convert_fusion
  42.8 0.1 copy.7
  42.9 0.2 reshape.42
  43.0 7.2 %all_gather.9 = bf16[960,256]{0,1:T(8,128)(2,1)S(1)} all-gather(bf16[960,64]{0,1:T(8,128)(2,1)S(1)} %reshape.42), channel_id=1, replica_groups=mesh['row'=8,'col'=4] {'col'}, dimensions={1}, use_global_device_ids=true | all-gather | bytes 614400 | tf_op jit(solution)/shard_map/all_gather | solution.py:66
  50.2 0.0 copy-start.1
  50.2 0.7 copy-done.1
  50.9 30.5 %all-gather = bf16[8,64,32]{1,2,0:T(8,128)(2,1)S(1)} all-gather(bf16[1,64,32]{1,2,0:T(8,128)(2,1)S(1)} %bitcast.20), channel_id=1, replica_groups=mesh['row'=8,'col'=4] {'row'}, dimensions={0}, use_global_device_ids=true | all-gather | bytes 36864 | tf_op jit(solution)/shard_map/all_gather | solution.py:70
  81.5 0.1 reshape.45
  81.6 0.6 fusion.16
  82.2 0.2 convolution_bitcast_fusion
  82.4 0.7 copy.10
  83.1 0.0 reduce-scatter.4.cloned.1.call-update
  83.1 0.0 copy-start.3
  83.2 0.6 copy-done.3
  83.8 0.6 dynamic-slice
  85.0 5.7 %all-reduce = f32[256]{0:T(256)S(1)} all-reduce(f32[256]{0:T(256)S(1)} %get-tuple-element.5), channel_id=3, replica_groups=mesh['row'=8,'col'=4] {'col'}, use_global_device_ids=true, to_apply=%region_3.4.clone | all-reduce | flops 256 | bytes 2048
  90.7 0.1 dynamic-slice.1
  90.8 12.3 %reduce-scatter.4.cloned.1.call-done = f32[64,32]{1,0:T(8,128)} async-done(((f32[256,32]{1,0:T(8,128)}), f32[64,32]{1,0:T(8,128)}) %reduce-scatter.4.cloned.1.call-update) | async-done | bytes 8208
  103.1 0.8 copy.11
  103.9 0.6 broadcast_divide_fusion
  (4 shorter events, 0.0 us)
Async XLA Ops:
  6.5 1.1 %copy-start = (bf16[5,192,64]{1,2,0:T(8,128)(2,1)S(1)}, bf16[5,192,64]{1,2,0:T(8,128)(2,1)}, u32[]{:S(2)}) copy-start(bf16[5,192,64]{1,2,0:T(8,128)(2,1)} %param.3) | copy-start | bytes 368644
  6.5 96.5 %reduce-scatter.4.cloned.1.call-start = ((), (), s32[]{:S(2)}) async-start(), calls=%async_computation.1 | async-start | bytes 163840
  8.1 34.6 %copy-start.2 = (f32[5]{0:T(128)S(1)}, f32[5]{0:T(128)}, u32[]{:S(2)}) copy-start(f32[5]{0:T(128)} %param.4) | copy-start | bytes 64
  50.2 0.7 copy-start.1
  83.1 0.7 copy-start.3
Sparse Core Ops, SparseCore 0:
  83.3 19.7 reduce-scatter.3
where the time goes:
time: 112 us; the launch traced here: 111 us
  blocking collectives  78 us (70%)
  between operations  14.1 us (13%)
  waiting for transfers between devices  12.3 us (11%)
  local copies, waits for them, and re-layouts  4.23 us (4%)
  other arithmetic  1.94 us (2%)
    all_gather x1, blocking collectives, shards(): lax.all_gather(unit, 'row', axis=1, tiled=True)  34.6 us
    all_gather x1, blocking collectives, shards(): lax.all_gather(vectors, 'row', axis=1, tiled=True)  30.5 us
    unnamed x2, waiting for transfers between devices  12.3 us
    all_gather x1, blocking collectives, shards(): own_panel = lax.all_gather(weighted, 'col', axis=1, tiled=True)  7.17 us
    unnamed x1, blocking collectives  5.67 us
    unnamed x13, local copies, waits for them, and re-layouts  3.68 us
  transfers between devices with their start and end apart: 1, of which 1 were waited for; matrix products, arithmetic and copies ran while one was open for 1% of the time, Pallas kernels for 0%

commit v1 on v0

--- a/solution.py
+++ b/solution.py
@@ -63,7 +63,13 @@
     def positions_of(panel):
         return jnp.arange(panel.shape[1], dtype=jnp.int32)
 
-    own_panel = lax.all_gather(weighted, "col", axis=1, tiled=True)
+    size = lax.axis_size("col")
+    current, blocks = (weighted, [weighted])
+    for _ in range(size - 1):
+        current = lax.ppermute(current, "col", [(i, (i + 1) % size) for i in range(size)])
+        blocks.insert(0, current)
+    line = jnp.concatenate(blocks, axis=1)
+    own_panel = jnp.roll(line, (lax.axis_index("col") + 1) * weighted.shape[1], axis=1)
     own_ids = row_index * (col_count * segments) + positions_of(own_panel)
     partner_panel, partner_vectors = (
         lax.all_gather(unit, "row", axis=1, tiled=True),

time: 112 us -> 110 us (0.982)
  blocking collectives: 78 us -> 70.7 us
  waiting for transfers between devices: 12.3 us -> 16.9 us
    all_gather x1 -> x0, blocking collectives: 7.17 us -> none  [shards(): own_panel = lax.all_gather(weighted, 'col', axis=1, tiled=True)]
    ppermute x0 -> x3, waiting for transfers between devices: none -> 4.31 us  [shards(): lax.ppermute(current, 'col', [(i, (i + 1) % size) for i in range(size)])]
    unnamed x13 -> x20, local copies, waits for them, and re-layouts: 3.68 us -> 4.26 us
  transfers between devices with their start and end apart: 1 -> 4, of which waited for: 1 -> 2; matrix products, arithmetic and copies ran while one was open for 1% -> 1% of each run, Pallas kernels for 0% -> 0%
where the time goes in v1:
time: 110 us
  blocking collectives  70.7 us (64%)
  waiting for transfers between devices  16.9 us (15%)
  between operations  14.2 us (13%)
  local copies, waits for them, and re-layouts  4.81 us (4%)
  other arithmetic  1.95 us (2%)
    all_gather x1, blocking collectives, shards(): lax.all_gather(unit, 'row', axis=1, tiled=True)  34.5 us
    all_gather x1, blocking collectives, shards(): lax.all_gather(vectors, 'row', axis=1, tiled=True)  30.5 us
    unnamed x2, waiting for transfers between devices  12.6 us
    unnamed x1, blocking collectives  5.67 us
    ppermute x3, waiting for transfers between devices, shards(): lax.ppermute(current, 'col', [(i, (i + 1) % size) for i in range(size)])  4.31 us
    unnamed x20, local copies, waits for them, and re-layouts  4.26 us
  transfers between devices with their start and end apart: 4, of which 2 were waited for; matrix products, arithmetic and copies ran while one was open for 1% of the time, Pallas kernels for 0%

profile of v1, /device:TPU:0, one launch (start us, length us, event | category | flops | bytes accessed | tf_op | source)
XLA Modules:
  0.0 109.9 jit_solution(11611013068902548754)
XLA Ops:
  6.5 0.0 copy-start
  6.5 0.0 reduce-scatter.4.cloned.1.call-start
  6.5 1.1 %fusion.3 = f32[5,64]{1,0:T(8,128)S(1)} fusion(bf16[5,192,64]{1,2,0:T(8,128)(2,1)} %param.3), kind=kLoop, calls=%fused_computation.7 | loop fusion | flops 184000 | bytes 124160 | tf_op jit(solution)/shard_map/reduce_sum | solution.py:12
  7.7 0.0 copy-done
  7.7 0.0 copy-start.2
  7.7 0.1 fusion.4
  7.8 0.5 copy-done.2
  8.3 0.1 multiply_convert_fusion
  8.4 0.1 copy.7
  8.5 0.2 reshape.42
  8.7 0.5 collective-permute-start
  9.2 0.1 copy.8
  9.3 0.2 reshape.43
  9.5 4.3 %collective-permute-done = bf16[960,64]{0,1:T(8,128)(2,1)S(1)} collective-permute-done((bf16[960,64]{0,1:T(8,128)(2,1)S(1)}, bf16[960,64]{0,1:T(8,128)(2,1)S(1)}, u32[]{:S(2)}, u32[]{:S(2)}) %collective-permute-start) | collective-permute-done | bytes 122912 | tf_op jit(solution)/shard_map/ppermute | solution.py:69
  13.8 0.0 collective-permute-start.1
  13.8 34.5 %all_gather.6 = bf16[960,512]{0,1:T(8,128)(2,1)S(1)} all-gather(bf16[960,64]{0,1:T(8,128)(2,1)S(1)} %reshape.43), channel_id=1, replica_groups=mesh['row'=8,'col'=4] {'row'}, dimensions={1}, use_global_device_ids=true | all-gather | bytes 1105920 | tf_op jit(solution)/shard_map/all_gather | solution.py:75
  48.3 0.0 copy-start.1
  48.3 0.0 collective-permute-done.1
  48.3 0.1 collective-permute-start.2
  48.4 0.6 copy-done.1
  49.0 30.5 %all-gather = bf16[8,64,32]{1,2,0:T(8,128)(2,1)S(1)} all-gather(bf16[1,64,32]{1,2,0:T(8,128)(2,1)S(1)} %bitcast.19), channel_id=1, replica_groups=mesh['row'=8,'col'=4] {'row'}, dimensions={0}, use_global_device_ids=true | all-gather | bytes 36864 | tf_op jit(solution)/shard_map/all_gather | solution.py:76
  79.6 0.1 reshape.45
  79.7 0.0 collective-permute-done.2
  79.9 0.6 fusion.18
  80.5 0.2 convolution_bitcast_fusion
  80.6 0.8 copy.10
  81.4 0.0 reduce-scatter.4.cloned.1.call-update
  81.4 0.0 copy-start.3
  81.4 0.6 copy-done.3
  82.1 0.6 dynamic-slice
  83.3 5.7 %all-reduce = f32[256]{0:T(256)S(1)} all-reduce(f32[256]{0:T(256)S(1)} %get-tuple-element.5), channel_id=3, replica_groups=mesh['row'=8,'col'=4] {'col'}, use_global_device_ids=true, to_apply=%region_3.4.clone | all-reduce | flops 256 | bytes 2048
  89.0 0.1 dynamic-slice.1
  89.1 12.6 %reduce-scatter.4.cloned.1.call-done = f32[64,32]{1,0:T(8,128)} async-done(((f32[256,32]{1,0:T(8,128)}), f32[64,32]{1,0:T(8,128)}) %reduce-scatter.4.cloned.1.call-update) | async-done | bytes 8208
  101.6 0.8 copy.11
  102.4 0.6 broadcast_divide_fusion
  (12 shorter events, 0.1 us)
Async XLA Ops:
  6.5 1.1 %copy-start = (bf16[5,192,64]{1,2,0:T(8,128)(2,1)S(1)}, bf16[5,192,64]{1,2,0:T(8,128)(2,1)}, u32[]{:S(2)}) copy-start(bf16[5,192,64]{1,2,0:T(8,128)(2,1)} %param.3) | copy-start | bytes 368644
  6.5 95.1 %reduce-scatter.4.cloned.1.call-start = ((), (), s32[]{:S(2)}) async-start(), calls=%async_computation.1 | async-start | bytes 163840
  7.7 0.7 copy-start.2
  8.7 5.1 %collective-permute-start = (bf16[960,64]{0,1:T(8,128)(2,1)S(1)}, bf16[960,64]{0,1:T(8,128)(2,1)S(1)}, u32[]{:S(2)}, u32[]{:S(2)}) collective-permute-start(bf16[960,64]{0,1:T(8,128)(2,1)S(1)} %reshape.42), channel_id=1, source_target_pairs={{0,1},{1,2},{2,3},{3,0},{4,5},{5,6},{6,7},{7,4},{8,9},{9,10},{10,1... | collective-permute-start | bytes 368648 | tf_op jit(solution)/shard_map/ppermute | solution.py:69
  13.8 34.5 %collective-permute-start.1 = (bf16[960,64]{0,1:T(8,128)(2,1)S(1)}, bf16[960,64]{0,1:T(8,128)(2,1)S(1)}, u32[]{:S(2)}, u32[]{:S(2)}) collective-permute-start(bf16[960,64]{0,1:T(8,128)(2,1)S(1)} %collective-permute-done), channel_id=1, source_target_pairs={{0,1},{1,2},{2,3},{3,0},{4,5},{5,6},{6,7},{7,4},{8,9},{9,10},{10,1... | collective-permute-start | bytes 368648 | tf_op jit(solution)/shard_map/ppermute | solution.py:69
  48.3 0.7 copy-start.1
  48.3 31.4 %collective-permute-start.2 = (bf16[960,64]{0,1:T(8,128)(2,1)S(1)}, bf16[960,64]{0,1:T(8,128)(2,1)S(1)}, u32[]{:S(2)}, u32[]{:S(2)}) collective-permute-start(bf16[960,64]{0,1:T(8,128)(2,1)S(1)} %collective-permute-done.1), channel_id=1, source_target_pairs={{0,1},{1,2},{2,3},{3,0},{4,5},{5,6},{6,7},{7,4},{8,9},{9,10},{10,1... | collective-permute-start | bytes 368648 | tf_op jit(solution)/shard_map/ppermute | solution.py:69
  81.4 0.7 copy-start.3
Sparse Core Ops, SparseCore 0:
  81.5 20.0 reduce-scatter.3
